TPU v7x, 256 devices: a whole 4x4x8 slice. The times are simulated.
256 devices in a mesh: wide: 16 (over x_hi, z), grp: 16 (over y, x_lo, core).
Axes of the slice: x: 4 (x_hi: 2, x_lo: 2; x = x_hi * 2 + x_lo), y: 4, z: 8, core: 2. Of those that a mesh axis runs over, the one named last changes fastest.
Arguments:
- rows_in: bfloat16 [8192, 7168], P('wide', 'grp'), may hold values from -6 to 6
- upstream: bfloat16 [8192, 7168], P('wide', 'grp'), may hold values from -1.5 to 1.5
- probs: float32 [8192], P('wide'), may hold values from 0.05 to 1
- route: int32 [8192, 1], P('wide'), may hold values from 0 to 15; in each aligned block of 512 rows (0 to 511, 512 to 1023, ...) at most 48 rows name the same one
- live: int32 [16], P('wide'), may hold values from 96 to 512, as said below
- gate_up: bfloat16 [16, 7168, 2048], P('wide', 'grp'), may hold values from -0.0625 to 0.0625
- down: bfloat16 [16, 1024, 7168], P('wide', None, 'grp'), may hold values from -0.1875 to 0.1875
Outputs:
- grad_rows: bfloat16 [8192, 7168], P('wide', 'grp')
- grad_prob: bfloat16 [8192], P('wide')
- grad_gate_up: bfloat16 [16, 7168, 2048], P('wide', 'grp')
- grad_down: bfloat16 [16, 1024, 7168], P('wide', None, 'grp')
Inputs may be any that keep to these rules, and one draw needn't show every extreme that they name: `route`: in each aligned block of 512 rows no expert is named by more than 48 rows, a bound that some block reaches; every expert is named somewhere. Some block is live in full.
All inputs are finite; a program needn't handle non-finite values.
Results may differ from a plain program's by a relative error of at most 0.01.
Values may be sent and summed in bfloat16 or wider, within the bound.
A program may use at most 128 MiB of HBM per device.

v0:
```python
import jax
import jax.numpy as jnp
from jax import lax
from jax.sharding import Mesh
from jax.sharding import PartitionSpec as P

GRP = ("grp_0", "grp_1", "grp_2")


BALANCE = 1.0


def copy_for_each(value, axis):
    copies = jnp.broadcast_to(value, (lax.axis_size(axis), *value.shape))
    return lax.all_to_all(copies, axis, split_axis=0, concat_axis=0, tiled=True)


def taken_together(value, axis):
    return copy_for_each(value, axis).sum(axis=0)


def sent_together(arrays, axis, split_dim, concat_dim, along):
    both = jnp.concatenate(arrays, axis=along)
    result, at, gathered = (
        lax.all_to_all(both, axis, split_axis=split_dim, concat_axis=concat_dim, tiled=True),
        0,
        [],
    )
    for a in arrays:
        gathered.append(lax.slice_in_dim(result, at, at + a.shape[along], axis=along))
        at += a.shape[along]
    return tuple(gathered)


def split_up(value, dim, devices):
    shape = value.shape
    tiles = value.reshape(*shape[:dim], devices, shape[dim] // devices, *shape[dim + 1 :])
    return jnp.moveaxis(tiles, dim, 0)


def sent_and_summed(value, axis, dim):
    tiles = split_up(value, dim, lax.axis_size(axis))
    arrived = lax.all_to_all(tiles, axis, split_axis=0, concat_axis=0, tiled=True)
    return arrived.sum(axis=0)


def summed_rows(value, axes, dim):
    far, near = axes
    own = sent_and_summed(split_up(value, dim, lax.axis_size(far)), near, dim + 1)
    return jnp.sum(lax.all_to_all(own, far, 0, 0, tiled=True), axis=0)


def sent_together_2(arrays, axis, dim, along):
    ends, at = ([], 0)
    for a in arrays[:-1]:
        at += a.shape[along]
        ends.append(at)
    both = jnp.concatenate(arrays, axis=along)
    return tuple(jnp.split(summed_rows(both, axis, dim), ends, axis=along))


def rows_first(arrays, axis, dims):
    turned = [jnp.moveaxis(a, dim, 0) for a, dim in zip(arrays, dims)]
    both = jnp.concatenate([t.reshape(len(t), -1) for t in turned], axis=1)
    result, at, gathered = (lax.all_gather(both, axis, axis=0, tiled=True), 0, [])
    for t, dim in zip(turned, dims):
        section = result[:, at : at + t[0].size].reshape(-1, *t.shape[1:])
        gathered.append(jnp.moveaxis(section, 0, dim))
        at += t[0].size
    return tuple(gathered)


def in_one_piece(arrays, axis, split_dim, concat_dim, along):
    columns = [a.reshape(*a.shape[:along], -1) for a in arrays]
    both = jnp.concatenate(columns, axis=along)
    result, at, gathered = (
        lax.all_to_all(both, axis, split_axis=split_dim, concat_axis=concat_dim, tiled=True),
        0,
        [],
    )
    for a, column in zip(arrays, columns):
        section = result[..., at : at + column.shape[along]]
        gathered.append(section.reshape(*section.shape[:along], *a.shape[along:]))
        at += column.shape[along]
    return tuple(gathered)


def activate(gate, up, grad_hidden):
    sigmoid_gate = jax.nn.sigmoid(gate)
    swish = gate * sigmoid_gate
    hidden = (swish * up).astype(jnp.bfloat16)
    grad_gate = (grad_hidden * up * sigmoid_gate * (1.0 + gate * (1.0 - sigmoid_gate))).astype(
        jnp.bfloat16
    )
    grad_up = (grad_hidden * swish).astype(jnp.bfloat16)
    return (hidden, grad_gate, grad_up)


def contract_rows(left, right):
    return lax.dot_general(
        left, right, (((0,), (0,)), ((), ())), preferred_element_type=jnp.float32
    )


def contract_last(left, right):
    return lax.dot_general(
        left, right, (((1,), (1,)), ((), ())), preferred_element_type=jnp.float32
    )


def arrange(values, selector):
    return jnp.dot(selector, values, preferred_element_type=jnp.float32).astype(jnp.bfloat16)


def on_device(rows_in, upstream, probs, route, live, gate_up, down):
    experts = lax.axis_size("wide")
    rows_dev = rows_in.shape[0]
    slice_width = rows_in.shape[1]
    hidden_width = down.shape[1]
    capacity = rows_dev * 3 // (2 * experts)
    slot_total = experts * capacity
    own_pair = gate_up[0]
    own_down = down[0]
    expert_of = route[:, 0]
    position = lax.iota(jnp.int32, rows_dev)
    inside = position < live[0]
    live_mask = inside.astype(jnp.float32)
    labels = lax.iota(jnp.int32, experts)
    onehot = (expert_of[:, None] == labels[None, :]).astype(jnp.int32)
    local_loads = jnp.sum(onehot * inside.astype(jnp.int32)[:, None], axis=0)
    global_loads = taken_together(local_loads, "wide").astype(jnp.float32)
    load_share = global_loads / rows_dev
    row_share = jnp.sum(onehot.astype(jnp.float32) * load_share[None, :], axis=1)
    slot_index = jnp.sum((jnp.cumsum(onehot, axis=0) - 1) * onehot, axis=1)
    target = expert_of * capacity + slot_index
    scaled = ((probs * live_mask)[:, None] * upstream.astype(jnp.float32)).astype(jnp.bfloat16)
    dispatch = (target[None, :] == lax.iota(jnp.int32, slot_total)[:, None]).astype(jnp.bfloat16)
    arrived = sent_together(
        (
            arrange(rows_in, dispatch).reshape(experts, capacity, slice_width),
            arrange(scaled, dispatch).reshape(experts, capacity, slice_width),
            arrange(upstream, dispatch).reshape(experts, capacity, slice_width),
        ),
        "wide",
        0,
        0,
        1,
    )
    token_rows = arrived[0].reshape(slot_total, slice_width)
    scaled_rows = arrived[1].reshape(slot_total, slice_width)
    upward_rows = arrived[2].reshape(slot_total, slice_width)
    preact = jnp.dot(token_rows, own_pair, preferred_element_type=jnp.float32)
    grad_partial = contract_last(scaled_rows, own_down)
    total_rows = preact.shape[0]
    shares = sent_together_2(
        (
            preact.reshape(total_rows, 2, hidden_width),
            grad_partial.reshape(total_rows, 1, hidden_width),
        ),
        (("grp_0", "grp_1"), "grp_2"),
        2,
        1,
    )
    piece_hidden, piece_gate, piece_up = activate(shares[0][:, 0], shares[0][:, 1], shares[1][:, 0])
    joined = rows_first(
        (piece_hidden[:, None, :], jnp.stack([piece_gate, piece_up], axis=1)), GRP, (2, 2)
    )
    hidden = joined[0][:, 0]
    grad_gate = joined[1][:, 0]
    grad_up = joined[1][:, 1]
    grad_pair = jnp.concatenate([grad_gate, grad_up], axis=1)
    grad_own = contract_last(grad_pair, own_pair)
    products = jnp.sum(
        jnp.dot(hidden, own_down, preferred_element_type=jnp.float32)
        * upward_rows.astype(jnp.float32),
        axis=1,
    )
    inner_sum = taken_together(products, GRP).astype(jnp.bfloat16)
    returned = in_one_piece(
        (
            grad_own.astype(jnp.bfloat16).reshape(experts, capacity, slice_width),
            inner_sum.reshape(experts, capacity),
        ),
        "wide",
        0,
        0,
        2,
    )
    grad_rows = contract_rows(dispatch, returned[0].reshape(slot_total, slice_width))
    inner_rows = contract_rows(dispatch, returned[1].reshape(slot_total, 1))[:, 0]
    pair_grad = contract_rows(token_rows, grad_pair)
    down_grad = contract_rows(hidden, scaled_rows)
    grad_prob = (live_mask * (inner_rows + BALANCE * row_share)).astype(jnp.bfloat16)
    return (
        grad_rows.astype(jnp.bfloat16),
        grad_prob,
        pair_grad.astype(jnp.bfloat16)[None],
        down_grad.astype(jnp.bfloat16)[None],
    )


def solution(mesh):
    finer = Mesh(
        mesh.devices.reshape(mesh.shape["wide"], 4, 2, 2), ("wide", "grp_0", "grp_1", "grp_2")
    )
    return jax.shard_map(
        on_device,
        mesh=finer,
        in_specs=(
            P("wide", GRP),
            P("wide", GRP),
            P("wide"),
            P("wide", None),
            P("wide"),
            P("wide", GRP, None),
            P("wide", None, GRP),
        ),
        out_specs=(P("wide", GRP), P("wide"), P("wide", GRP, None), P("wide", None, GRP)),
        check_vma=False,
    )
```

profile of v0, /device:TPU:1, one launch (start us, length us, event | category | flops | bytes accessed | tf_op | source)
XLA Modules:
  0.0 308.4 jit_solution(6345695939405275654)
XLA Ops:
  7.9 0.7 fusion.31
  8.6 1.1 reduce-window.6
  10.0 0.9 select_reduce_fusion
  10.9 0.7 multiply_add_fusion
  11.5 0.7 fusion.33
  12.2 1.6 fusion.12
  13.8 1.7 fusion.11
  15.8 0.6 fusion.10
  16.9 1.7 pad_maximum_fusion.2
  18.7 11.6 %all-to-all-start = ((bf16[16,144,448]{2,1,0:T(8,128)(2,1)}), bf16[16,144,448]{2,1,0:T(8,128)(2,1)S(1)}, u32[]{:S(2)}, u32[]{:S(2)}) async-start(bf16[16,144,448]{2,1,0:T(8,128)(2,1)} %pad_maximum_fusion.2), calls=%async_computation | async-start | bytes 4718592 | tf_op jit(solution)/shard_map/all_to_all | solution.py:25
  30.3 3.3 %copy.115 = bf16[56,8,16,128]{3,2,1,0:T(8,128)(2,1)} copy(bf16[56,8,16,128]{3,1,2,0:T(8,128)(2,1)} %bitcast.111) | data formatting | bytes 3670016
  33.7 1.2 copy.116
  34.8 51.6 %all-to-all-done = bf16[16,144,448]{2,1,0:T(8,128)(2,1)S(1)} async-done(((bf16[16,144,448]{2,1,0:T(8,128)(2,1)}), bf16[16,144,448]{2,1,0:T(8,128)(2,1)S(1)}, u32[]{:S(2)}, u32[]{:S(2)}) %all-to-all-start) | async-done | bytes 2064416 | tf_op jit(solution)/shard_map/all_to_all | solution.py:25
  86.4 1.1 fusion.37
  87.5 0.7 copy-done.4
  88.2 2.0 fusion.3
  90.2 1.1 convolution_bitcast_fusion
  91.3 0.9 pad_maximum_fusion
  92.2 1.1 copy.125
  93.3 14.2 %all_to_all.32 = f32[2,8,768,3,64]{2,4,1,3,0:T(8,128)} all-to-all(f32[2,8,768,3,64]{2,4,1,3,0:T(8,128)S(1)} %bitcast.105), channel_id=1, replica_groups=mesh['wide'=16,'grp_0'=4,'grp_1'=2,'grp_2'=2] {'grp_2'}, dimensions={0} | all-to-all | bytes 18874368 | tf_op jit(solution)/shard_map/all_to_all | solution.py:43
  107.5 7.1 %reduce_sum.73 = f32[8,768,3,64]{1,3,0,2:T(8,128)} reduce(f32[2,8,768,3,64]{2,4,1,3,0:T(8,128)} %all_to_all.32, f32[]{:T(128)} %constant.18.clone.1), dimensions={0}, to_apply=%region_3.0 | reduce | flops 1179648 | bytes 14155780 | tf_op jit(solution)/shard_map/reduce_sum | solution.py:44
  114.7 2.8 copy.96
  117.4 58.3 %all_to_all.33 = f32[8,768,3,64]{1,3,2,0:T(8,128)} all-to-all(f32[8,768,3,64]{1,3,2,0:T(8,128)S(1)} %copy.96), channel_id=1, replica_groups=mesh['wide'=16,'grp_0'=4,'grp_1'=2,'grp_2'=2] {'grp_0','grp_1'}, dimensions={0} | all-to-all | bytes 9437184 | tf_op jit(solution)/shard_map/all_to_all | solution.py:50
  175.7 2.7 reduce_sum.74
  178.5 0.4 copy.97
  179.2 0.9 copy.99
  180.5 0.5 copy.102
  181.0 37.7 %all-gather.2.cloned.1.call-done = bf16[1024,2304]{1,0:T(8,128)(2,1)} async-done(((bf16[64,2304]{1,0:T(8,128)(2,1)}), bf16[1024,2304]{1,0:T(8,128)(2,1)}) %all-gather.2.cloned.1.call-update) | async-done | bytes 4718608 | tf_op jit(solution)/shard_map/all_gather | solution.py:65
  218.6 3.8 %slice.59 = bf16[1024,1536]{1,0:T(8,128)(2,1)} slice(bf16[1024,2304]{1,0:T(8,128)(2,1)} %all-gather.2.cloned.1.call-done), slice={[0:1024], [768:2304]} | slice | bytes 6291456 | tf_op jit(solution)/shard_map/slice | solution.py:67
  222.4 4.7 %copy.100 = bf16[1024,1536]{0,1:T(8,128)(2,1)} copy(bf16[1024,1536]{1,0:T(8,128)(2,1)} %slice.59) | data formatting | bytes 6291456 | tf_op jit(solution)/shard_map/slice | solution.py:67
  227.1 5.7 %reshape.134 = bf16[1024,768,2]{0,2,1:T(2,128)(2,1)} reshape(bf16[1024,1536]{0,1:T(8,128)(2,1)} %copy.100) | data formatting | bytes 6291456 | tf_op jit(solution)/shard_map/reshape | solution.py:67
  232.8 9.6 %fusion.36 = (bf16[768,1,1024]{2,1,0:T(2,128)(2,1)}, bf16[768,1,1024]{2,1,0:T(2,128)(2,1)}) fusion(bf16[768,2,1024]{2,1,0:T(2,128)(2,1)} %bitcast.106), kind=kLoop, calls=%fused_computation.67 | loop fusion | bytes 6291456 | tf_op jit(solution)/shard_map/slice | solution.py:169
  242.4 2.3 fusion.17
  244.7 0.6 broadcast_in_dim.8
  245.3 4.1 %all-to-all-start.3 = ((f32[16,1,768]{2,1,0:T(1,128)}), f32[16,1,768]{2,1,0:T(1,128)S(1)}, u32[]{:S(2)}, u32[]{:S(2)}) async-start(f32[16,1,768]{2,1,0:T(1,128)} %broadcast_in_dim.8), calls=%async_computation.3 | async-start | bytes 98304 | tf_op jit(solution)/shard_map/all_to_all | solution.py:15
  249.4 4.2 %copy_bitcast_fusion.1 = (bf16[768,1024]{1,0:T(8,128)(2,1)S(1)}, bf16[768,1024]{1,0:T(8,128)(2,1)S(1)}) fusion(bf16[768,1,1024]{2,1,0:T(2,128)(2,1)} %get-tuple-element.7, bf16[768,1,1024]{2,1,0:T(2,128)(2,1)} %get-tuple-element.6), kind=kLoop, calls=%fused_computation.12 | loop fusion | bytes 6291456
  253.7 1.2 copy-done.5
  254.8 1.6 fusion.13
  256.8 0.6 broadcast_in_dim.9
  257.4 9.0 %all-to-all-start.5 = ((s32[16,1,16]{2,1,0:T(1,128)}), s32[16,1,16]{2,1,0:T(1,128)S(1)}, u32[]{:S(2)}, u32[]{:S(2)}) async-start(s32[16,1,16]{2,1,0:T(1,128)} %broadcast_in_dim.9), calls=%async_computation.5 | async-start | bytes 16384 | tf_op jit(solution)/shard_map/all_to_all | solution.py:15
  266.8 1.1 pad_maximum_fusion.7
  267.8 7.3 %all-to-all-done.5 = s32[16,1,16]{2,1,0:T(1,128)S(1)} async-done(((s32[16,1,16]{2,1,0:T(1,128)}), s32[16,1,16]{2,1,0:T(1,128)S(1)}, u32[]{:S(2)}, u32[]{:S(2)}) %all-to-all-start.5) | async-done | bytes 1056 | tf_op jit(solution)/shard_map/all_to_all | solution.py:15
  275.1 3.6 %all-to-all-start.4 = ((bf16[16,48,449]{2,1,0:T(8,128)(2,1)}), bf16[16,48,449]{2,1,0:T(8,128)(2,1)S(1)}, u32[]{:S(2)}, u32[]{:S(2)}) async-start(bf16[16,48,449]{2,1,0:T(8,128)(2,1)} %pad_maximum_fusion.7), calls=%async_computation.4 | async-start | bytes 1572864 | tf_op jit(solution)/shard_map/all_to_all | solution.py:77
  278.9 3.5 %fusion.16 = bf16[1,1024,448]{1,2,0:T(8,128)(2,1)} fusion(bf16[768,448]{1,0:T(8,128)(2,1)} %bitcast.120, bf16[1024,2304]{1,0:T(8,128)(2,1)} %all-gather.2.cloned.1.call-done), kind=kOutput, calls=%fused_computation.26 | convolution fusion | flops 705101824 | bytes 3276800 | tf_op jit(solution)/shard_map/dot_general | solution.py:100
  282.3 4.5 %fusion = bf16[1,448,2048]{2,1,0:T(8,128)(2,1)} fusion(bf16[768,448]{1,0:T(8,128)(2,1)} %bitcast.118, bf16[768,1024]{1,0:T(8,128)(2,1)S(1)} %get-tuple-element.14, bf16[768,1024]{1,0:T(8,128)(2,1)} %copy-done.5), kind=kOutput, calls=%fused_computation.4 | convolution fusion | flops 1416495104 | bytes 5668864 | tf_op jit(solution)/shard_map/dot_general | solution.py:100
  286.9 12.0 %all-to-all-done.4 = bf16[16,48,449]{2,1,0:T(8,128)(2,1)S(1)} async-done(((bf16[16,48,449]{2,1,0:T(8,128)(2,1)}), bf16[16,48,449]{2,1,0:T(8,128)(2,1)S(1)}, u32[]{:S(2)}, u32[]{:S(2)}) %all-to-all-start.4) | async-done | bytes 689696 | tf_op jit(solution)/shard_map/all_to_all | solution.py:77
  298.8 1.4 fusion.18
  300.9 0.6 select_convert_fusion
  (46 shorter events, 3.4 us)
Async XLA Ops:
  7.2 8.6 %copy-start = (bf16[512,448]{0,1:T(8,128)(2,1)S(1)}, bf16[512,448]{0,1:T(8,128)(2,1)}, u32[]{:S(2)}) copy-start(bf16[512,448]{0,1:T(8,128)(2,1)} %param.7) | copy-start | bytes 1376260
  18.7 67.7 %all-to-all-start = ((bf16[16,144,448]{2,1,0:T(8,128)(2,1)}), bf16[16,144,448]{2,1,0:T(8,128)(2,1)S(1)}, u32[]{:S(2)}, u32[]{:S(2)}) async-start(bf16[16,144,448]{2,1,0:T(8,128)(2,1)} %pad_maximum_fusion.2), calls=%async_computation | async-start | bytes 4718592 | tf_op jit(solution)/shard_map/all_to_all | solution.py:25
  30.3 188.4 %all-gather.2.cloned.1.call-start = ((), (), s32[]{:S(2)}) async-start(), calls=%async_computation.6 | async-start | bytes 5013504 | tf_op jit(solution)/shard_map/all_gather | solution.py:65
  30.3 3.4 %copy-start.6 = (bf16[1,1024,448]{1,2,0:T(8,128)(2,1)S(1)}, bf16[1,1024,448]{1,2,0:T(8,128)(2,1)}, u32[]{:S(2)}) copy-start(bf16[1,1024,448]{1,2,0:T(8,128)(2,1)} %param.13) | copy-start | bytes 2752516
  86.4 1.8 copy-start.4
  87.5 2.7 copy-start.9
  87.5 2.7 copy-start.10
  88.2 2.0 copy-start.8
  178.4 1.8 copy-start.2
  232.8 9.6 %copy-start.7 = (bf16[1,1024,448]{1,2,0:T(8,128)(2,1)S(1)}, bf16[1,1024,448]{1,2,0:T(8,128)(2,1)}, u32[]{:S(2)}) copy-start(bf16[1,1024,448]{1,2,0:T(8,128)(2,1)} %param.13) | copy-start | bytes 2752516
  245.3 11.4 %all-to-all-start.3 = ((f32[16,1,768]{2,1,0:T(1,128)}), f32[16,1,768]{2,1,0:T(1,128)S(1)}, u32[]{:S(2)}, u32[]{:S(2)}) async-start(f32[16,1,768]{2,1,0:T(1,128)} %broadcast_in_dim.8), calls=%async_computation.3 | async-start | bytes 98304 | tf_op jit(solution)/shard_map/all_to_all | solution.py:15
  249.4 5.4 %copy-start.3 = (bf16[1,448,2048]{2,1,0:T(8,128)(2,1)S(1)}, bf16[1,448,2048]{2,1,0:T(8,128)(2,1)}, u32[]{:S(2)}) copy-start(bf16[1,448,2048]{2,1,0:T(8,128)(2,1)} %param.12) | copy-start | bytes 5505028
  253.7 1.2 copy-start.5
  256.5 22.3 %copy-start.11 = (s32[512,1]{0,1:T(1,128)S(1)}, s32[512,1]{0,1:T(1,128)}, u32[]{:S(2)}) copy-start(s32[512,1]{0,1:T(1,128)} %param.10) | copy-start | bytes 6148
  257.4 17.7 %all-to-all-start.5 = ((s32[16,1,16]{2,1,0:T(1,128)}), s32[16,1,16]{2,1,0:T(1,128)S(1)}, u32[]{:S(2)}, u32[]{:S(2)}) async-start(s32[16,1,16]{2,1,0:T(1,128)} %broadcast_in_dim.9), calls=%async_computation.5 | async-start | bytes 16384 | tf_op jit(solution)/shard_map/all_to_all | solution.py:15
  275.1 23.7 %all-to-all-start.4 = ((bf16[16,48,449]{2,1,0:T(8,128)(2,1)}), bf16[16,48,449]{2,1,0:T(8,128)(2,1)S(1)}, u32[]{:S(2)}, u32[]{:S(2)}) async-start(bf16[16,48,449]{2,1,0:T(8,128)(2,1)} %pad_maximum_fusion.7), calls=%async_computation.4 | async-start | bytes 1572864 | tf_op jit(solution)/shard_map/all_to_all | solution.py:77
  282.3 19.2 %copy-start.1 = (bf16[512,448]{0,1:T(8,128)(2,1)S(1)}, bf16[512,448]{0,1:T(8,128)(2,1)}, u32[]{:S(2)}) copy-start(bf16[512,448]{0,1:T(8,128)(2,1)} %param.7) | copy-start | bytes 1376260
Sparse Core Ops, SparseCore 0:
  180.3 38.2 all-gather.1
where the time goes:
time: 312 us; the launch traced here: 308 us
  waiting for transfers between devices  109 us (35%)
  blocking collectives  72.5 us (23%)
  local copies, waits for them, and re-layouts  44.6 us (14%)
  starting transfers between devices  28.3 us (9%)
  matrix products  20.5 us (7%)
  other arithmetic  18.9 us (6%)
  between operations  15 us (5%)
    all_to_all x1, blocking collectives, summed_rows(): return jnp.sum(lax.all_to_all(own, far, 0, 0, tiled=True), axis=0)  58.3 us
    all_to_all x1, waiting for transfers between devices, sent_together(): lax.all_to_all(both, axis, split_axis=split_dim, concat_axis=concat_dim,...  51.6 us
    all_gather x1, waiting for transfers between devices, rows_first(): lax.all_gather(both, axis, axis=0, tiled=True)  37.7 us
    all_to_all x1, blocking collectives, sent_and_summed(): lax.all_to_all(tiles, axis, split_axis=0, concat_axis=0, tiled=True)  14.2 us
    all_to_all x2, starting transfers between devices, copy_for_each(): return lax.all_to_all(copies, axis, split_axis=0, concat_axis=0, tiled=True)  13 us
    all_to_all x1, waiting for transfers between devices, in_one_piece(): lax.all_to_all(both, axis, split_axis=split_dim, concat_axis=concat_dim,...  12 us
    all_to_all x1, starting transfers between devices, sent_together(): lax.all_to_all(both, axis, split_axis=split_dim, concat_axis=concat_dim,...  11.6 us
    unnamed x27, local copies, waits for them, and re-layouts  10.7 us
  transfers between devices with their start and end apart: 5, of which 4 were waited for; matrix products, arithmetic and copies ran while one was open for 7% of the time, Pallas kernels for 0%

commit v1 on v0

v1 whole, which is shorter than its diff:
```python
import functools

import jax
import jax.numpy as jnp
from jax import lax
from jax.experimental import pallas as pl
from jax.experimental.pallas import tpu as pltpu
from jax.sharding import PartitionSpec as P

F32 = jnp.float32
BF16 = jnp.bfloat16
MESH = pl.DeviceIdType.MESH
BALANCE = 1.0
CHUNKS = 3
LANES = 128


def product(left, right, left_dim, right_dim):
    return lax.dot_general(
        left, right, (((left_dim,), (right_dim,)), ((), ())), preferred_element_type=F32
    )


def await_bytes(ref, sem):
    pltpu.make_async_copy(ref, ref, sem).wait()


def kernel(
    experts,
    live_ref,
    rows_ref,
    upstream_ref,
    probs_ref,
    route_ref,
    pair_hbm,
    down_hbm,
    grad_rows_ref,
    grad_prob_ref,
    grad_pair_ref,
    grad_down_ref,
    padded_rows,
    padded_up,
    select,
    outgoing,
    incoming,
    w_pair,
    w_down_raw,
    w_down,
    own_sum,
    core_out,
    core_in,
    y_out,
    y_in,
    x_own,
    x_out,
    x_in,
    joined,
    ret_out,
    ret_in,
    rows_acc,
    pair_acc,
    down_acc,
    count_out,
    count_in,
    w_sem,
    count_s,
    count_r,
    disp_s,
    disp_r,
    core_s,
    core_r,
    y_s,
    y_r,
    x_s,
    x_r,
    gx_s,
    gx_r,
    gy_s,
    gy_r,
    gc_s,
    gc_r,
    ret_s,
    ret_r,
):
    rows, width = rows_ref.shape
    chunks, _, slots, packed = outgoing.shape
    hidden = down_hbm.shape[0]
    padded = padded_rows.shape[1]
    spare = padded - width
    both = experts // 2
    chunk_rows = experts * slots
    half_rows = both * slots

    w = lax.axis_index("wide")
    g = lax.axis_index("grp")
    core = lax.rem(g, 2)
    place = lax.div(g, 2)
    xl = lax.rem(place, 2)
    y = lax.div(place, 2)
    other_core = g + 1 - 2 * core
    other_x = g + 2 - 4 * xl
    ys = [lax.rem(y + k, 4) for k in range(4)]

    z = lax.rem(w, 8)
    xh = lax.div(w, 8)
    wides = []
    for dx, dz in [(0, 4), (1, 4), (0, 3), (0, 5), (1, 3), (1, 5), (0, 2), (0, 6), (1, 2), (1, 6),
                   (0, 1), (0, 7), (1, 1), (1, 7), (1, 0)]:
        wides.append(lax.rem(xh + dx, 2) * 8 + lax.rem(z + dz, 8))

    barrier = pltpu.get_barrier_semaphore()

    def greet(to_w, to_g):
        pl.semaphore_signal(barrier, inc=1, device_id=(to_w, to_g), device_id_type=MESH)

    for to in wides:
        greet(to, g)
    greet(w, other_core)
    greet(w, other_x)
    for k in (1, 2, 3):
        greet(w, ys[k] * 4 + xl * 2 + core)

    pair_copy = pltpu.make_async_copy(pair_hbm, w_pair.at[pl.ds(0, width)], w_sem.at[0])
    pair_copy.start()
    down_copy = pltpu.make_async_copy(down_hbm, w_down_raw, w_sem.at[1])
    down_copy.start()

    expert_row = route_ref[...]
    position = lax.broadcasted_iota(jnp.int32, (1, rows), 1)
    inside = position < live_ref[0]
    labels = lax.broadcasted_iota(jnp.int32, (experts, rows), 0)
    onehot = jnp.where((labels == expert_row) & inside, 1.0, 0.0).astype(F32)
    earlier = jnp.where(
        lax.broadcasted_iota(jnp.int32, (rows, rows), 0)
        < lax.broadcasted_iota(jnp.int32, (rows, rows), 1),
        1.0,
        0.0,
    ).astype(BF16)
    before = product(onehot.astype(BF16), earlier, 1, 0)
    rank = jnp.sum(before * onehot, axis=0, keepdims=True)
    counts = jnp.sum(onehot, axis=1, keepdims=True)
    count_out[...] = jnp.broadcast_to(counts, count_out.shape)
    expert_f = expert_row.astype(F32)
    probs_row = probs_ref[...]

    padded_rows[:, pl.ds(0, width)] = rows_ref[...]
    padded_rows[:, pl.ds(width, spare)] = jnp.zeros((rows, spare), BF16)
    padded_up[:, pl.ds(0, width)] = upstream_ref[...]
    padded_up[:, pl.ds(width, spare)] = jnp.zeros((rows, spare), BF16)
    shift_rows = 128

    @pl.loop(0, rows // shift_rows)
    def _(i):
        at = pl.ds(pl.multiple_of(i * shift_rows, shift_rows), shift_rows)
        padded_up[at, :] = pltpu.roll(padded_up[at, :].astype(F32), spare, 1).astype(BF16)

    def remote(src, dst, send, recv, to_w, to_g):
        return pltpu.make_async_remote_copy(
            src_ref=src, dst_ref=dst, send_sem=send, recv_sem=recv,
            device_id=(to_w, to_g), device_id_type=MESH,
        )

    edge = packed - padded
    for c in range(chunks):
        offset = rank - float(c * slots)
        fits = inside & (offset >= 0.0) & (offset < float(slots))
        target = jnp.where(fits, expert_f * float(slots) + offset, -1.0)
        index = lax.broadcasted_iota(jnp.int32, (chunk_rows, rows), 0).astype(F32)
        chosen = jnp.where(index == target, 1.0, 0.0).astype(F32)
        slot_prob = jnp.sum(chosen * probs_row, axis=1, keepdims=True)
        chosen = chosen.astype(BF16)
        select[c] = chosen
        row_part = product(chosen, padded_rows[...], 1, 0).astype(BF16)
        up_part = (slot_prob * product(chosen, padded_up[...], 1, 0)).astype(BF16)
        outgoing[c, :, :, pl.ds(0, edge)] = row_part[:, :edge].reshape(experts, slots, edge)
        outgoing[c, :, :, pl.ds(edge, padded - edge)] = (
            row_part[:, edge:] + up_part[:, : padded - edge]
        ).reshape(experts, slots, padded - edge)
        outgoing[c, :, :, pl.ds(padded, packed - padded)] = up_part[:, padded - edge :].reshape(
            experts, slots, packed - padded
        )
        incoming[c, lax.rem(w, 2), lax.div(w, 2)] = outgoing[c, w]
        if c == 0:
            pl.semaphore_wait(barrier, len(wides) + 5)
        for to in wides:
            remote(
                outgoing.at[c, to],
                incoming.at[c, lax.rem(w, 2), lax.div(w, 2)],
                disp_s.at[c], disp_r.at[c], to, g,
            ).start()
    count_in[w] = count_out[...]
    for to in wides:
        remote(count_out, count_in.at[w], count_s, count_r, to, g).start()

    pair_copy.wait()
    w_pair[pl.ds(width, spare), :] = jnp.zeros((spare, w_pair.shape[1]), BF16)
    down_copy.wait()
    w_down[:, pl.ds(0, width)] = w_down_raw[...]
    w_down[:, pl.ds(width, spare)] = jnp.zeros((hidden, spare), BF16)

    @pl.loop(0, hidden // shift_rows)
    def _(i):
        at = pl.ds(pl.multiple_of(i * shift_rows, shift_rows), shift_rows)
        w_down[at, :] = pltpu.roll(w_down[at, :].astype(F32), spare, 1).astype(BF16)

    tile = 512

    def contract(c):
        await_bytes(outgoing.at[c, pl.ds(0, len(wides))], disp_r.at[c])

        def partial(part, keep):
            left = incoming[c, part, :, :, pl.ds(0, padded)].reshape(half_rows, padded)
            right = incoming[c, part, :, :, pl.ds(edge, padded)].reshape(half_rows, padded)

            @pl.loop(0, 2 * hidden // tile)
            def _(n):
                at = pl.ds(pl.multiple_of(n * tile, tile), tile)
                keep(at, product(left, w_pair[:, at], 1, 0).reshape(both, slots, tile))

            @pl.loop(0, hidden // tile)
            def _(n):
                at = pl.ds(pl.multiple_of(n * tile, tile), tile)
                to = pl.ds(pl.multiple_of(2 * hidden + n * tile, tile), tile)
                keep(to, product(right, w_down[at, :], 1, 1).reshape(both, slots, tile))

        def keep_out(at, value):
            core_out[c, :, :, at] = value.astype(BF16)

        partial(1 - core, keep_out)
        remote(core_out.at[c], core_in.at[c], core_s.at[c], core_r.at[c], w, other_core).start()

        def keep_own(at, value):
            own_sum[c, :, :, at] = value

        partial(core, keep_own)

    def reduce_y(c):
        await_bytes(core_in.at[c], core_r.at[c])
        for k in (2, 1, 3):
            at = pl.ds(2 * ys[k], 2)
            y_out[c, k - 1] = (own_sum[c, at] + core_in[c, at].astype(F32)).astype(BF16)
            remote(
                y_out.at[c, k - 1], y_in.at[c, k - 1], y_s.at[c], y_r.at[c],
                w, ys[k] * 4 + xl * 2 + core,
            ).start()

    def reduce_x(c):
        await_bytes(y_in.at[c], y_r.at[c])

        def total(part):
            at = 2 * y + part
            value = own_sum[c, at] + core_in[c, at].astype(F32)
            for k in range(3):
                value = value + y_in[c, k, part].astype(F32)
            return value

        x_out[c] = total(1 - xl).astype(BF16)
        remote(x_out.at[c], x_in.at[c], x_s.at[c], x_r.at[c], w, other_x).start()
        x_own[c] = total(xl)

    def send_on(c, at):
        for k in (2, 1, 3):
            remote(
                joined.at[c, core, at], joined.at[c, core, at], gy_s.at[c], gy_r.at[c],
                w, ys[k] * 4 + xl * 2 + core,
            ).start()

    def activate(c):
        await_bytes(x_in.at[c], x_r.at[c])
        value = x_own[c] + x_in[c].astype(F32)
        gate = value[:, :hidden]
        up = value[:, hidden : 2 * hidden]
        grad_hidden = value[:, 2 * hidden :]
        sigmoid_gate = jax.nn.sigmoid(gate)
        swish = gate * sigmoid_gate
        act = (swish * up).astype(BF16)
        grad_gate = grad_hidden * up * sigmoid_gate * (1.0 + gate * (1.0 - sigmoid_gate))
        joined[c, core, place, :, pl.ds(0, hidden)] = act
        joined[c, core, place, :, pl.ds(hidden, hidden)] = grad_gate.astype(BF16)
        joined[c, core, place, :, pl.ds(2 * hidden, hidden)] = (grad_hidden * swish).astype(BF16)
        inner = jnp.sum(act.astype(F32) * grad_hidden, axis=1, keepdims=True)
        high = inner.astype(BF16).astype(F32)
        lane = lax.broadcasted_iota(jnp.int32, (slots, LANES), 1)
        at = width - (padded - LANES)
        split = jnp.where(lane == at, high, jnp.where(lane == at + 1, inner - high, 0.0))
        joined[c, core, place, :, pl.ds(3 * hidden, LANES)] = split.astype(BF16)
        remote(
            joined.at[c, core, place], joined.at[c, core, place], gx_s.at[c], gx_r.at[c], w, other_x
        ).start()
        send_on(c, place)

    def forward(c):
        await_bytes(joined.at[c, 0, 0], gx_r.at[c])
        send_on(c, 2 * y + 1 - xl)

    def share(c):
        await_bytes(joined.at[c, 0, pl.ds(0, 6)], gy_r.at[c])
        remote(
            joined.at[c, core], joined.at[c, core], gc_s.at[c], gc_r.at[c], w, other_core
        ).start()

    def give_back(c):
        await_bytes(joined.at[c, 0], gc_r.at[c])

        @pl.loop(0, 2)
        def _(part):
            pairs = joined[c, part, :, :, pl.ds(hidden, 2 * hidden)].reshape(half_rows, 2 * hidden)
            inner = joined[c, part, :, :, pl.ds(3 * hidden, LANES)].reshape(half_rows, LANES)
            value = product(pairs, w_pair[...], 1, 1)
            cut = padded - LANES
            ret_out[c, part, :, :, pl.ds(0, cut)] = (
                value[:, :cut].astype(BF16).reshape(both, slots, cut)
            )
            ret_out[c, part, :, :, pl.ds(cut, LANES)] = (
                value[:, cut:].astype(BF16) + inner
            ).reshape(both, slots, LANES)

        ret_in[c, w] = ret_out[c, lax.rem(w, 2), lax.div(w, 2)]
        for to in wides:
            remote(
                ret_out.at[c, lax.rem(to, 2), lax.div(to, 2)], ret_in.at[c, w],
                ret_s.at[c], ret_r.at[c], to, g,
            ).start()

    def weigh(c):
        left = incoming[c, :, :, :, pl.ds(0, padded)].reshape(chunk_rows, padded)
        right = incoming[c, :, :, :, pl.ds(edge, padded)].reshape(chunk_rows, padded)
        step = 256

        @pl.loop(0, 2 * hidden // step)
        def _(n):
            at = pl.ds(pl.multiple_of(n * step, step), step)
            src = pl.ds(pl.multiple_of(hidden + n * step, step), step)
            value = product(left, joined[c, :, :, :, src].reshape(chunk_rows, step), 0, 0)
            if c > 0:
                value = value + pair_acc[:, at]
            if c == chunks - 1:
                grad_pair_ref[:, at] = value[:width].astype(BF16)
            else:
                pair_acc[:, at] = value

        @pl.loop(0, hidden // step)
        def _(n):
            at = pl.ds(pl.multiple_of(n * step, step), step)
            value = product(joined[c, :, :, :, at].reshape(chunk_rows, step), right, 0, 0)
            if c > 0:
                value = value + down_acc[at, :]
            if c == chunks - 1:
                grad_down_ref[at, :] = value.astype(BF16)
            else:
                down_acc[at, :] = value

    def receive(c, inner):
        await_bytes(outgoing.at[c, pl.ds(0, len(wides)), :, pl.ds(0, padded)], ret_r.at[c])
        back = ret_in[c].reshape(chunk_rows, padded)
        chosen = select[c]
        value = product(chosen, back, 0, 0)
        if c > 0:
            value = value + rows_acc[...]
        if c == chunks - 1:
            grad_rows_ref[...] = value[:, :width].astype(BF16)
        else:
            rows_acc[...] = value
        return inner + product(back[:, padded - LANES :], chosen, 0, 0)

    contract(0)
    reduce_y(0)
    contract(1)
    reduce_y(1)
    reduce_x(0)
    activate(0)
    forward(0)
    contract(2)
    reduce_y(2)
    reduce_x(1)
    activate(1)
    share(0)
    forward(1)
    give_back(0)
    weigh(0)
    reduce_x(2)
    activate(2)
    share(1)
    forward(2)
    give_back(1)
    weigh(1)
    share(2)
    give_back(2)
    weigh(2)
    inner = jnp.zeros((LANES, rows), F32)
    for c in range(chunks):
        inner = receive(c, inner)

    await_bytes(count_in.at[pl.ds(0, len(wides))], count_r)
    loads = jnp.sum(count_in[...], axis=0)[:, :1]
    share_row = jnp.sum(
        jnp.where(labels == expert_row, 1.0, 0.0) * (loads * (1.0 / rows)), axis=0, keepdims=True
    )
    at = width - (padded - LANES)
    inner_row = (inner[at : at + 1] + inner[at + 1 : at + 2]) / probs_row
    inner_row = inner_row.astype(BF16).astype(F32)
    grad_prob_ref[...] = jnp.where(inside, inner_row + BALANCE * share_row, 0.0).astype(BF16)

    await_bytes(count_in.at[pl.ds(0, len(wides))], count_s)
    for c in range(chunks):
        await_bytes(outgoing.at[c, pl.ds(0, len(wides))], disp_s.at[c])
        await_bytes(core_out.at[c], core_s.at[c])
        await_bytes(y_out.at[c], y_s.at[c])
        await_bytes(x_out.at[c], x_s.at[c])
        await_bytes(joined.at[c, 0, 0], gx_s.at[c])
        await_bytes(joined.at[c, 0, pl.ds(0, 6)], gy_s.at[c])
        await_bytes(joined.at[c, 0], gc_s.at[c])
        await_bytes(outgoing.at[c, pl.ds(0, len(wides)), :, pl.ds(0, padded)], ret_s.at[c])


def on_device(rows_in, upstream, probs, route, live, gate_up, down):
    rows, width = rows_in.shape
    experts = lax.axis_size("wide")
    hidden = down.shape[1]
    slots = rows * 3 // (2 * experts) // CHUNKS
    padded = -(-width // LANES) * LANES
    packed = 2 * width
    both = experts // 2
    total = 3 * hidden
    vmem = pltpu.VMEM
    dma = pltpu.SemaphoreType.DMA
    each = dma((CHUNKS,))
    scratch = [
        vmem((rows, padded), BF16),
        vmem((rows, padded), BF16),
        vmem((CHUNKS, experts * slots, rows), BF16),
        vmem((CHUNKS, experts, slots, packed), BF16),
        vmem((CHUNKS, 2, both, slots, packed), BF16),
        vmem((padded, 2 * hidden), BF16),
        vmem((hidden, width), BF16),
        vmem((hidden, padded), BF16),
        vmem((CHUNKS, both, slots, total), F32),
        vmem((CHUNKS, both, slots, total), BF16),
        vmem((CHUNKS, both, slots, total), BF16),
        vmem((CHUNKS, 3, 2, slots, total), BF16),
        vmem((CHUNKS, 3, 2, slots, total), BF16),
        vmem((CHUNKS, slots, total), F32),
        vmem((CHUNKS, slots, total), BF16),
        vmem((CHUNKS, slots, total), BF16),
        vmem((CHUNKS, 2, both, slots, total + LANES), BF16),
        vmem((CHUNKS, 2, both, slots, padded), BF16),
        vmem((CHUNKS, experts, slots, padded), BF16),
        vmem((rows, padded), F32),
        vmem((padded, 2 * hidden), F32),
        vmem((hidden, padded), F32),
        vmem((experts, LANES), F32),
        vmem((experts, experts, LANES), F32),
        dma((2,)),
        dma,
        dma,
    ] + [each] * 16
    in_vmem = pl.BlockSpec(memory_space=pltpu.VMEM)
    out = pl.pallas_call(
        functools.partial(kernel, experts),
        out_shape=(
            jax.ShapeDtypeStruct((rows, width), BF16),
            jax.ShapeDtypeStruct((1, rows), BF16),
            jax.ShapeDtypeStruct((width, 2 * hidden), BF16),
            jax.ShapeDtypeStruct((hidden, padded), BF16),
        ),
        in_specs=[
            pl.BlockSpec(memory_space=pltpu.SMEM),
            in_vmem,
            in_vmem,
            in_vmem,
            in_vmem,
            pl.BlockSpec(memory_space=pl.ANY),
            pl.BlockSpec(memory_space=pl.ANY),
        ],
        out_specs=(in_vmem,) * 4,
        scratch_shapes=scratch,
        compiler_params=pltpu.CompilerParams(
            collective_id=0, has_side_effects=True, vmem_limit_bytes=60 * 2**20
        ),
    )(
        live,
        rows_in,
        upstream,
        probs.reshape(1, rows),
        route.reshape(1, rows),
        gate_up[0],
        down[0],
    )
    grad_rows, grad_prob, grad_pair, grad_down = out
    return (
        grad_rows,
        grad_prob.reshape(rows),
        grad_pair[None],
        grad_down[None, :, padded - width :],
    )


def solution(mesh):
    return jax.shard_map(
        on_device,
        mesh=mesh,
        in_specs=(
            P("wide", "grp"),
            P("wide", "grp"),
            P("wide"),
            P("wide", None),
            P("wide"),
            P("wide", "grp", None),
            P("wide", None, "grp"),
        ),
        out_specs=(P("wide", "grp"), P("wide"), P("wide", "grp", None), P("wide", None, "grp")),
        check_vma=False,
    )
```

time: 312 us -> 118 us (0.38); the launches traced: 308 us -> 118 us
  waiting for transfers between devices: 109 us -> 0 us
  Pallas kernels: 0 us -> 104 us
  blocking collectives: 72.5 us -> 0 us
  local copies, waits for them, and re-layouts: 44.6 us -> 11.7 us
  starting transfers between devices: 28.3 us -> 0 us
  matrix products: 20.5 us -> 0 us
  other arithmetic: 18.9 us -> 1.22 us
  between operations: 15 us -> 1.38 us
    pallas_call x0 -> x1, Pallas kernels: none -> 104 us  [on_device(): pl.pallas_call(functools.partial(kernel, experts), out_shape=(jax.ShapeDt...]
    all_to_all x2 -> x0, blocking collectives: 72.5 us -> none  [the longest x1 58.3 us: summed_rows(): return jnp.sum(lax.all_to_all(own, far, 0, 0, tiled=True), axis=0)]
    all_to_all x4 -> x0, waiting for transfers between devices: 70.8 us -> none  [the longest x1 51.6 us: sent_together(): lax.all_to_all(both, axis, split_axis=split_dim, concat_axis=concat_dim,...]
    all_gather x1 -> x0, waiting for transfers between devices: 37.7 us -> none  [rows_first(): lax.all_gather(both, axis, axis=0, tiled=True)]
    all_to_all x4 -> x0, starting transfers between devices: 28.2 us -> none  [the longest x2 13 us: copy_for_each(): return lax.all_to_all(copies, axis, split_axis=0, concat_axis=0, tiled=True)]
    dot_general x11 -> x0, matrix products: 20.5 us -> none  [the longest x4 9.73 us: contract_rows(): lax.dot_general(left, right, (((0,), (0,)), ((), ())), preferred_element_...]
    slice x6 -> x0, local copies, waits for them, and re-layouts: 19.6 us -> none  [the longest x1 9.56 us: on_device(): grad_gate = joined[1][:, 0]]
    reduce_sum x6 -> x0, other arithmetic: 10.9 us -> none  [the longest x1 7.14 us: sent_and_summed(): return arrived.sum(axis=0)]
  transfers between devices with their start and end apart: 5 -> 0, of which waited for: 4 -> 0; matrix products, arithmetic and copies ran while one was open for 7% -> 0% of each run, Pallas kernels for 0% -> 0%
where the time goes in v1:
time: 118 us
  Pallas kernels  104 us (88%)
  local copies, waits for them, and re-layouts  11.7 us (10%)
  between operations  1.38 us (1%)
  other arithmetic  1.22 us (1%)
    pallas_call x1, Pallas kernels, on_device(): pl.pallas_call(functools.partial(kernel, experts), out_shape=(jax.ShapeDt...  104 us
    unnamed x10, local copies, waits for them, and re-layouts  9.86 us

profile of v1, /device:TPU:1, one launch (start us, length us, event | category | flops | bytes accessed | tf_op | source)
XLA Modules:
  0.0 118.1 jit_solution(14346342072698037333)
XLA Ops:
  0.6 0.0 copy-start.1
  1.4 2.0 %copy.12.rows_ref = bf16[512,448]{1,0:T(8,128)(2,1)} copy(bf16[512,448]{0,1:T(8,128)(2,1)} %param.7) | data formatting | bytes 917504 | tf_op args[0]
  3.4 2.0 %copy.13.upstream_ref = bf16[512,448]{1,0:T(8,128)(2,1)} copy(bf16[512,448]{0,1:T(8,128)(2,1)} %param.8) | data formatting | bytes 917504 | tf_op args[1]
  5.4 0.0 copy-done.1
  5.4 1.3 %copy.11 = bf16[1,1024,448]{2,1,0:T(8,128)(2,1)} copy(bf16[1,1024,448]{1,2,0:T(8,128)(2,1)S(1)} %copy-done.1) | data formatting | bytes 1835008 | tf_op args[6]
  6.7 103.8 %shard_map.102 = (bf16[512,448]{1,0:T(8,128)(2,1)}, bf16[1,512]{1,0:T(2,128)(2,1)}, bf16[448,2048]{1,0:T(8,128)(2,1)}, bf16[1024,512]{1,0:T(8,128)(2,1)}) custom-call(s32[1]{0:T(128)S(6)} %copy.17.live_ref, bf16[512,448]{1,0:T(8,128)(2,1)} %copy.12.rows_ref, bf16[512,448]{1,0:T(8,128)(2,1)} %copy.13.upstream_ref, f32[1,512]{1,0:T(1,128)} %bitcast.10, ...), custom_call_target="tpu_custom_call" | custom-call | tf_op jit(solution)/shard_map/pallas_call | solution.py:458
  110.5 2.0 %copy.14 = bf16[512,448]{0,1:T(8,128)(2,1)} copy(bf16[512,448]{1,0:T(8,128)(2,1)} %get-tuple-element.12) | data formatting | bytes 917504
  112.5 1.2 %reduce = bf16[512]{0:T(512)(128)(2,1)} reduce(bf16[1,512]{1,0:T(2,128)(2,1)} %get-tuple-element.9, bf16[]{:T(256)} %constant.3), dimensions={0}, to_apply=%get-tuple-element.9.reduce_sub_computation | reduce | bytes 2050 | tf_op jit(solution)/shard_map/pallas_call | solution.py:458
  113.7 0.0 copy-start
  113.7 1.8 %slice_bitcast_fusion = bf16[1,1024,448]{2,1,0:T(8,128)(2,1)S(1)} fusion(bf16[1024,512]{1,0:T(8,128)(2,1)} %get-tuple-element.11), kind=kLoop, calls=%fused_computation | loop fusion | bytes 1835008 | tf_op jit(solution)/shard_map/broadcast_in_dim | solution.py:494
  115.6 1.3 %copy.15 = bf16[1,1024,448]{1,2,0:T(8,128)(2,1)} copy(bf16[1,1024,448]{2,1,0:T(8,128)(2,1)S(1)} %slice_bitcast_fusion) | data formatting | bytes 1835008
  116.8 0.0 copy-done
  116.8 1.2 %copy.18 = bf16[1,448,2048]{2,1,0:T(8,128)(2,1)} copy(bf16[1,448,2048]{2,1,0:T(8,128)(2,1)S(1)} %bitcast.9) | data formatting | bytes 3670016
Async XLA Ops:
  0.6 4.8 %copy-start.1 = (bf16[1,1024,448]{1,2,0:T(8,128)(2,1)S(1)}, bf16[1,1024,448]{1,2,0:T(8,128)(2,1)}, u32[]{:S(2)}) copy-start(bf16[1,1024,448]{1,2,0:T(8,128)(2,1)} %param.13) | copy-start | bytes 2752516
  113.7 3.1 %copy-start = (bf16[448,2048]{1,0:T(8,128)(2,1)S(1)}, bf16[448,2048]{1,0:T(8,128)(2,1)}, u32[]{:S(2)}) copy-start(bf16[448,2048]{1,0:T(8,128)(2,1)} %get-tuple-element.10) | copy-start | bytes 5505028

commit v2 on v1

v2 whole, which is shorter than its diff:
```python
import functools

import jax
import jax.numpy as jnp
from jax import lax
from jax.experimental import pallas as pl
from jax.experimental.pallas import tpu as pltpu
from jax.sharding import PartitionSpec as P

F32 = jnp.float32
BF16 = jnp.bfloat16
MESH = pl.DeviceIdType.MESH
BALANCE = 1.0
PARTS = (2, 2, 1, 1)
LANES = 128


def product(left, right, left_dim, right_dim):
    return lax.dot_general(
        left, right, (((left_dim,), (right_dim,)), ((), ())), preferred_element_type=F32
    )


def await_bytes(ref, sem, name="wait"):
    with jax.named_scope(name):
        pltpu.make_async_copy(ref, ref, sem).wait()


def kernel(
    experts,
    live_ref,
    rows_hbm,
    upstream_hbm,
    probs_ref,
    route_ref,
    pair_hbm,
    down_hbm,
    rows_vm,
    grad_prob_ref,
    pair_vm,
    down_vm,
    padded_rows,
    padded_up,
    select,
    outgoing,
    incoming,
    w_pair,
    w_down,
    own_sum,
    core_out,
    core_in,
    far_out,
    far_in,
    y_out,
    y_in,
    x_own,
    x_out,
    x_in,
    joined,
    ret_out,
    ret_in,
    rows_acc,
    count_out,
    count_in,
    w_sem,
    count_s,
    count_r,
    disp_s,
    disp_r,
    core_s,
    core_r,
    far_s,
    far_r,
    y_s,
    y_r,
    x_s,
    x_r,
    gx_s,
    gx_r,
    gy_s,
    gy_r,
    gz_s,
    gz_r,
    gf_s,
    gf_r,
    gc_s,
    gc_r,
    ret_s,
    ret_r,
):
    width, rows = rows_hbm.shape
    chunks = len(outgoing)
    packed = outgoing[0].shape[2]
    sizes = [ref.shape[1] for ref in outgoing]
    firsts = [sum(sizes[:c]) for c in range(chunks)]
    hidden = down_hbm.shape[1]
    padded = padded_rows.shape[0]
    spare = padded - width
    both = experts // 2

    w = lax.axis_index("wide")
    g = lax.axis_index("grp")
    core = lax.rem(g, 2)
    place = lax.div(g, 2)
    xl = lax.rem(place, 2)
    y = lax.div(place, 2)
    other_core = g + 1 - 2 * core
    other_x = g + 2 - 4 * xl
    ys = [lax.rem(y + k, 4) for k in range(4)]

    z = lax.rem(w, 8)
    xh = lax.div(w, 8)
    wides = []
    for dx, dz in [(0, 4), (1, 4), (0, 3), (0, 5), (1, 3), (1, 5), (0, 2), (0, 6), (1, 2), (1, 6),
                   (0, 1), (0, 7), (1, 1), (1, 7), (1, 0)]:
        wides.append(lax.rem(xh + dx, 2) * 8 + lax.rem(z + dz, 8))

    barrier = pltpu.get_barrier_semaphore()

    def greet(to_w, to_g):
        pl.semaphore_signal(barrier, inc=1, device_id=(to_w, to_g), device_id_type=MESH)

    for to in wides:
        greet(to, g)
    greet(w, other_core)
    greet(w, other_x)
    for k in (1, 3):
        greet(w, ys[k] * 4 + xl * 2 + core)

    into = (
        padded_rows.at[pl.ds(0, width)],
        padded_up.at[pl.ds(spare, width)],
        w_pair.at[pl.ds(0, width)],
        w_down.at[pl.ds(spare, width)],
    )
    copies = [
        pltpu.make_async_copy(src, dst, w_sem.at[i])
        for i, (src, dst) in enumerate(zip((rows_hbm, upstream_hbm, pair_hbm, down_hbm), into))
    ]
    for copy in copies:
        copy.start()
    padded_rows[pl.ds(width, spare), :] = jnp.zeros((spare, rows), BF16)
    padded_up[pl.ds(0, spare), :] = jnp.zeros((spare, rows), BF16)
    w_pair[pl.ds(width, spare), :] = jnp.zeros((spare, w_pair.shape[1]), BF16)
    w_down[pl.ds(0, spare), :] = jnp.zeros((spare, hidden), BF16)

    expert_row = route_ref[...]
    position = lax.broadcasted_iota(jnp.int32, (1, rows), 1)
    inside = position < live_ref[0]
    labels = lax.broadcasted_iota(jnp.int32, (experts, rows), 0)
    onehot = jnp.where((labels == expert_row) & inside, 1.0, 0.0).astype(F32)
    earlier = jnp.where(
        lax.broadcasted_iota(jnp.int32, (rows, rows), 0)
        < lax.broadcasted_iota(jnp.int32, (rows, rows), 1),
        1.0,
        0.0,
    ).astype(BF16)
    before = product(onehot.astype(BF16), earlier, 1, 0)
    rank = jnp.sum(before * onehot, axis=0, keepdims=True)
    counts = jnp.sum(onehot, axis=1, keepdims=True)
    count_out[...] = jnp.broadcast_to(counts, count_out.shape)
    expert_f = expert_row.astype(F32)
    probs_row = probs_ref[...]

    with jax.named_scope("load"):
        copies[0].wait()
        copies[1].wait()

    def remote(src, dst, send, recv, to_w, to_g):
        return pltpu.make_async_remote_copy(
            src_ref=src, dst_ref=dst, send_sem=send, recv_sem=recv,
            device_id=(to_w, to_g), device_id_type=MESH,
        )

    edge = packed - padded
    for c in range(chunks):
        slots = sizes[c]
        chunk_rows = experts * slots
        with jax.named_scope(f"arrange{c}"):
            offset = rank - float(firsts[c])
            fits = inside & (offset >= 0.0) & (offset < float(slots))
            target = jnp.where(fits, expert_f * float(slots) + offset, -1.0)
            index = lax.broadcasted_iota(jnp.int32, (chunk_rows, rows), 0).astype(F32)
            chosen = jnp.where(index == target, 1.0, 0.0).astype(F32)
            slot_prob = jnp.sum(chosen * probs_row, axis=1, keepdims=True)
            chosen = chosen.astype(BF16)
            select[c][...] = chosen
            row_part = product(chosen, padded_rows[...], 1, 1).astype(BF16)
            up_part = (slot_prob * product(chosen, padded_up[...], 1, 1)).astype(BF16)
            outgoing[c][:, :, pl.ds(0, edge)] = row_part[:, :edge].reshape(experts, slots, edge)
            outgoing[c][:, :, pl.ds(edge, padded - edge)] = (
                row_part[:, edge:] + up_part[:, : padded - edge]
            ).reshape(experts, slots, padded - edge)
            outgoing[c][:, :, pl.ds(padded, packed - padded)] = up_part[:, padded - edge :].reshape(
                experts, slots, packed - padded
            )
            incoming[c][lax.rem(w, 2), lax.div(w, 2)] = outgoing[c][w]
        if c == 0:
            with jax.named_scope("barrier"):
                pl.semaphore_wait(barrier, len(wides) + 4)
        with jax.named_scope(f"send{c}"):
            for to in wides:
                remote(
                    outgoing[c].at[to],
                    incoming[c].at[lax.rem(w, 2), lax.div(w, 2)],
                    disp_s.at[c], disp_r.at[c], to, g,
                ).start()
    count_in[w] = count_out[...]
    for to in wides:
        remote(count_out, count_in.at[w], count_s, count_r, to, g).start()

    with jax.named_scope("load2"):
        copies[2].wait()
        copies[3].wait()

    tile = 512

    def contract(c):
        slots = sizes[c]
        half_rows = both * slots
        await_bytes(outgoing[c].at[pl.ds(0, len(wides))], disp_r.at[c])

        def partial(parts, keep):
            def operand(first):
                blocks = [incoming[c][part, :, :, pl.ds(first, padded)] for part in parts]
                return jnp.concatenate(
                    [block.reshape(half_rows, padded) for block in blocks], axis=0
                )

            left, right = operand(0), operand(edge)

            @pl.loop(0, 2 * hidden // tile)
            def _(n):
                at = pl.ds(pl.multiple_of(n * tile, tile), tile)
                keep(at, product(left, w_pair[:, at], 1, 0))

            @pl.loop(0, hidden // tile)
            def _(n):
                at = pl.ds(pl.multiple_of(n * tile, tile), tile)
                to = pl.ds(pl.multiple_of(2 * hidden + n * tile, tile), tile)
                keep(to, product(right, w_down[:, at], 1, 0))

        def keep_out(at, value):
            core_out[c][:, :, at] = value[:half_rows].reshape(both, slots, tile).astype(BF16)

        def keep_own(at, value):
            own_sum[c][:, :, at] = value[-half_rows:].reshape(both, slots, tile)

        def keep_both(at, value):
            keep_out(at, value)
            keep_own(at, value)

        def exchange():
            remote(core_out[c], core_in[c], core_s.at[c], core_r.at[c], w, other_core).start()

        if half_rows < LANES:
            partial((1 - core, core), keep_both)
            exchange()
        else:
            partial((1 - core,), keep_out)
            exchange()
            partial((core,), keep_own)

    def to_y(k, src, dst, send, recv):
        remote(src, dst, send, recv, w, ys[k] * 4 + xl * 2 + core).start()

    def partial_sum(c, k, part):
        at = 2 * ys[k] + part
        return own_sum[c][at] + core_in[c][at].astype(F32)

    def reduce_y(c):
        await_bytes(core_in[c], core_r.at[c])
        for side in (0, 1):
            far_out[c][side] = partial_sum(c, 2, side).astype(BF16)
            to_y((1, 3)[side], far_out[c].at[side], far_in[c].at[side], far_s.at[c], far_r.at[c])
        for side in (0, 1):
            y_out[c][side, 1 - side] = partial_sum(c, (1, 3)[side], 1 - side).astype(BF16)
            to_y(
                (1, 3)[side], y_out[c].at[side, 1 - side], y_in[c].at[side, 1 - side],
                y_s.at[c], y_r.at[c],
            )

    def relay_y(c):
        await_bytes(far_in[c], far_r.at[c])
        for side in (0, 1):
            value = partial_sum(c, (1, 3)[side], side) + far_in[c][side].astype(F32)
            y_out[c][side, side] = value.astype(BF16)
            to_y(
                (1, 3)[side], y_out[c].at[side, side], y_in[c].at[side, side], y_s.at[c], y_r.at[c]
            )

    def reduce_x(c):
        await_bytes(y_in[c], y_r.at[c])

        def total(part):
            value = partial_sum(c, 0, part)
            for side in (0, 1):
                value = value + y_in[c][side, part].astype(F32)
            return value

        x_out[c][...] = total(1 - xl).astype(BF16)
        remote(x_out[c], x_in[c], x_s.at[c], x_r.at[c], w, other_x).start()
        x_own[c][...] = total(xl)

    def activate(c):
        slots = sizes[c]
        await_bytes(x_in[c], x_r.at[c])
        value = x_own[c][...] + x_in[c][...].astype(F32)
        gate = value[:, :hidden]
        up = value[:, hidden : 2 * hidden]
        grad_hidden = value[:, 2 * hidden :]
        sigmoid_gate = jax.nn.sigmoid(gate)
        swish = gate * sigmoid_gate
        act = (swish * up).astype(BF16)
        grad_gate = grad_hidden * up * sigmoid_gate * (1.0 + gate * (1.0 - sigmoid_gate))
        joined[c][core, place, :, pl.ds(0, hidden)] = act
        joined[c][core, place, :, pl.ds(hidden, hidden)] = grad_gate.astype(BF16)
        joined[c][core, place, :, pl.ds(2 * hidden, hidden)] = (grad_hidden * swish).astype(BF16)
        inner = jnp.sum(act.astype(F32) * grad_hidden, axis=1, keepdims=True)
        high = inner.astype(BF16).astype(F32)
        lane = lax.broadcasted_iota(jnp.int32, (slots, LANES), 1)
        at = width - (padded - LANES)
        split = jnp.where(lane == at, high, jnp.where(lane == at + 1, inner - high, 0.0))
        joined[c][core, place, :, pl.ds(3 * hidden, LANES)] = split.astype(BF16)
        for k in (1, 3):
            piece_to_y(c, k, place, gy_s, gy_r)
        remote(
            joined[c].at[core, place], joined[c].at[core, place], gx_s.at[c], gx_r.at[c], w, other_x
        ).start()

    def piece_to_y(c, k, at, send, recv):
        piece = joined[c].at[core, at]
        to_y(k, piece, piece, send.at[c], recv.at[c])

    def forward(c):
        await_bytes(joined[c].at[0, 0], gx_r.at[c])
        for k in (1, 3):
            piece_to_y(c, k, 2 * y + 1 - xl, gz_s, gz_r)

    def pass_near(c):
        await_bytes(joined[c].at[0, pl.ds(0, 2)], gy_r.at[c])
        piece_to_y(c, 1, 2 * ys[3] + xl, gf_s, gf_r)

    def pass_far(c):
        await_bytes(joined[c].at[0, pl.ds(0, 2)], gz_r.at[c])
        piece_to_y(c, 3, 2 * ys[1] + 1 - xl, gf_s, gf_r)
        for k in (0, 1, 3):
            share(c, k)

    def share(c, k):
        pieces = joined[c].at[core, pl.ds(2 * ys[k], 2)]
        remote(pieces, pieces, gc_s.at[c], gc_r.at[c], w, other_core).start()

    def share_last(c):
        await_bytes(joined[c].at[0, pl.ds(0, 2)], gf_r.at[c])
        share(c, 2)

    def give_back(c):
        slots = sizes[c]
        half_rows = both * slots
        await_bytes(joined[c].at[0], gc_r.at[c])
        cut = padded - LANES
        for part in (0, 1):
            pairs = joined[c][part, :, :, pl.ds(hidden, 2 * hidden)].reshape(half_rows, 2 * hidden)
            inner = joined[c][part, :, :, pl.ds(3 * hidden, LANES)].reshape(half_rows, LANES)
            value = product(pairs, w_pair[...], 1, 1)
            ret_out[c][part, :, :, pl.ds(0, cut)] = (
                value[:, :cut].astype(BF16).reshape(both, slots, cut)
            )
            ret_out[c][part, :, :, pl.ds(cut, LANES)] = (
                value[:, cut:].astype(BF16) + inner
            ).reshape(both, slots, LANES)
        ret_in[c][w] = ret_out[c][lax.rem(w, 2), lax.div(w, 2)]
        for to in wides:
            remote(
                ret_out[c].at[lax.rem(to, 2), lax.div(to, 2)], ret_in[c].at[w],
                ret_s.at[c], ret_r.at[c], to, g,
            ).start()

    def weigh():
        step = 256
        lefts, rights = [], []
        for c in range(chunks):
            chunk_rows = experts * sizes[c]
            lefts.append(incoming[c][:, :, :, pl.ds(0, padded)].reshape(chunk_rows, padded).T)
            rights.append(incoming[c][:, :, :, pl.ds(edge, padded)].reshape(chunk_rows, padded).T)

        def total(parts, at):
            value = 0.0
            for c in range(chunks):
                right = joined[c][:, :, :, at].reshape(experts * sizes[c], step)
                value = value + product(parts[c], right, 1, 0)
            return value

        @pl.loop(0, 2 * hidden // step)
        def _(n):
            at = pl.ds(pl.multiple_of(n * step, step), step)
            src = pl.ds(pl.multiple_of(hidden + n * step, step), step)
            pair_vm[:, at] = total(lefts, src)[:width].astype(BF16)

        @pl.loop(0, hidden // step)
        def _(n):
            at = pl.ds(pl.multiple_of(n * step, step), step)
            down_vm[:, at] = total(rights, at)[spare:].astype(BF16)

    def receive(c):
        chunk_rows = experts * sizes[c]
        await_bytes(outgoing[c].at[pl.ds(0, len(wides)), :, pl.ds(0, padded)], ret_r.at[c])
        value = product(ret_in[c][...].reshape(chunk_rows, padded), select[c][...], 0, 0)
        rows_acc[...] = value if c == 0 else rows_acc[...] + value

    order = (
        (contract, 0), (reduce_y, 0), (relay_y, 0), (reduce_x, 0), (contract, 1), (reduce_y, 1),
        (activate, 0), (relay_y, 1), (contract, 2), (reduce_y, 2), (forward, 0), (pass_near, 0),
        (contract, 3), (reduce_y, 3), (reduce_x, 1), (relay_y, 2), (pass_far, 0), (activate, 1),
        (relay_y, 3), (share_last, 0), (forward, 1), (reduce_x, 2), (give_back, 0), (activate, 2),
        (pass_near, 1), (pass_far, 1), (reduce_x, 3), (activate, 3), (forward, 2),
        (share_last, 1), (forward, 3), (give_back, 1), (pass_near, 2), (pass_near, 3),
        (pass_far, 2), (pass_far, 3), (share_last, 2), (share_last, 3), (give_back, 2),
        (give_back, 3),
    )
    for stage, c in order:
        with jax.named_scope(stage.__name__ + str(c)):
            stage(c)
    with jax.named_scope("weigh"):
        weigh()
    for c in range(chunks):
        with jax.named_scope(f"receive{c}"):
            receive(c)
    rows_vm[...] = rows_acc[pl.ds(0, width), :].astype(BF16)

    await_bytes(count_in.at[pl.ds(0, len(wides))], count_r)
    loads = jnp.sum(count_in[...], axis=0)[:, :1]
    share_row = jnp.sum(
        jnp.where(labels == expert_row, 1.0, 0.0) * (loads * (1.0 / rows)), axis=0, keepdims=True
    )
    inner = rows_acc[pl.ds(width, 8), :]
    inner_row = (inner[0:1] + inner[1:2]) / probs_row
    inner_row = inner_row.astype(BF16).astype(F32)
    grad_prob_ref[...] = jnp.where(inside, inner_row + BALANCE * share_row, 0.0)

    await_bytes(count_in.at[pl.ds(0, len(wides))], count_s)
    for c in range(chunks):
        await_bytes(outgoing[c].at[pl.ds(0, len(wides))], disp_s.at[c])
        await_bytes(core_out[c], core_s.at[c])
        await_bytes(far_out[c], far_s.at[c])
        await_bytes(y_out[c], y_s.at[c])
        await_bytes(x_out[c], x_s.at[c])
        await_bytes(joined[c].at[0, 0], gx_s.at[c])
        for sem in (gy_s, gz_s, gf_s):
            await_bytes(joined[c].at[0, pl.ds(0, 2)], sem.at[c])
        await_bytes(joined[c].at[0], gc_s.at[c])
        await_bytes(outgoing[c].at[pl.ds(0, len(wides)), :, pl.ds(0, padded)], ret_s.at[c])


def store_kernel(rows_vm, prob_vm, pair_vm, down_vm, rows_hbm, prob_ref, pair_hbm, down_hbm, sem):
    copies = [
        pltpu.make_async_copy(src, dst, sem.at[i])
        for i, (src, dst) in enumerate(((pair_vm, pair_hbm), (down_vm, down_hbm), (rows_vm, rows_hbm)))
    ]
    for copy in copies:
        copy.start()
    prob_ref[...] = prob_vm[...].reshape(prob_ref.shape).astype(BF16)
    for copy in copies:
        copy.wait()


def on_device(rows_in, upstream, probs, route, live, gate_up, down):
    rows, width = rows_in.shape
    experts = lax.axis_size("wide")
    hidden = down.shape[1]
    unit = rows * 3 // (2 * experts) // sum(PARTS)
    sizes = [part * unit for part in PARTS]
    chunks = len(sizes)
    padded = -(-width // LANES) * LANES
    packed = 2 * width
    both = experts // 2
    total = 3 * hidden
    vmem = pltpu.VMEM
    dma = pltpu.SemaphoreType.DMA
    each = dma((chunks,))
    scratch = [
        vmem((padded, rows), BF16),
        vmem((padded, rows), BF16),
        [vmem((experts * slots, rows), BF16) for slots in sizes],
        [vmem((experts, slots, packed), BF16) for slots in sizes],
        [vmem((2, both, slots, packed), BF16) for slots in sizes],
        vmem((padded, 2 * hidden), BF16),
        vmem((padded, hidden), BF16),
        [vmem((both, slots, total), F32) for slots in sizes],
        [vmem((both, slots, total), BF16) for slots in sizes],
        [vmem((both, slots, total), BF16) for slots in sizes],
        [vmem((2, slots, total), BF16) for slots in sizes],
        [vmem((2, slots, total), BF16) for slots in sizes],
        [vmem((2, 2, slots, total), BF16) for slots in sizes],
        [vmem((2, 2, slots, total), BF16) for slots in sizes],
        [vmem((slots, total), F32) for slots in sizes],
        [vmem((slots, total), BF16) for slots in sizes],
        [vmem((slots, total), BF16) for slots in sizes],
        [vmem((2, both, slots, total + LANES), BF16) for slots in sizes],
        [vmem((2, both, slots, padded), BF16) for slots in sizes],
        [vmem((experts, slots, padded), BF16) for slots in sizes],
        vmem((padded, rows), F32),
        vmem((experts, LANES), F32),
        vmem((experts, experts, LANES), F32),
        dma((4,)),
        dma,
        dma,
    ] + [each] * 22
    in_vmem = pl.BlockSpec(memory_space=pltpu.VMEM)
    anywhere = pl.BlockSpec(memory_space=pltpu.HBM)
    out = pl.pallas_call(
        functools.partial(kernel, experts),
        out_shape=(
            vmem((width, rows), BF16),
            vmem((1, rows), F32),
            vmem((width, 2 * hidden), BF16),
            vmem((width, hidden), BF16),
        ),
        in_specs=[
            pl.BlockSpec(memory_space=pltpu.SMEM),
            anywhere,
            anywhere,
            in_vmem,
            in_vmem,
            anywhere,
            anywhere,
        ],
        out_specs=(in_vmem,) * 4,
        scratch_shapes=scratch,
        compiler_params=pltpu.CompilerParams(
            collective_id=0, has_side_effects=True, vmem_limit_bytes=121 * 2**19
        ),
    )(
        live,
        rows_in.T,
        upstream.T,
        probs.reshape(1, rows),
        route.reshape(1, rows),
        gate_up[0],
        down[0].T,
    )
    grad_rows, grad_prob, grad_pair, grad_down = pl.pallas_call(
        store_kernel,
        out_shape=(
            jax.ShapeDtypeStruct((width, rows), BF16),
            jax.ShapeDtypeStruct((rows,), BF16),
            jax.ShapeDtypeStruct((width, 2 * hidden), BF16),
            jax.ShapeDtypeStruct((width, hidden), BF16),
        ),
        in_specs=[in_vmem] * 4,
        out_specs=(anywhere, in_vmem, anywhere, anywhere),
        scratch_shapes=[dma((3,))],
        compiler_params=pltpu.CompilerParams(vmem_limit_bytes=2**20),
    )(*out)
    return (
        grad_rows.T,
        grad_prob,
        grad_pair[None],
        grad_down.T[None],
    )


def solution(mesh):
    return jax.shard_map(
        on_device,
        mesh=mesh,
        in_specs=(
            P("wide", "grp"),
            P("wide", "grp"),
            P("wide"),
            P("wide", None),
            P("wide"),
            P("wide", "grp", None),
            P("wide", None, "grp"),
        ),
        out_specs=(P("wide", "grp"), P("wide"), P("wide", "grp", None), P("wide", None, "grp")),
        check_vma=False,
    )
```

time: 118 us -> 100 us (0.85)
  local copies, waits for them, and re-layouts: 11.7 us -> 0 us
  Pallas kernels: 104 us -> 98.6 us
  other arithmetic: 1.22 us -> 0 us
    unnamed x10 -> x0, local copies, waits for them, and re-layouts: 9.86 us -> none
    pallas_call x1 -> x2, Pallas kernels: 104 us -> 98.6 us  [the longest x1 96.4 us: on_device(): pl.pallas_call(functools.partial(kernel, experts), out_shape=(vmem((width...]
    broadcast_in_dim x1 -> x0, local copies, waits for them, and re-layouts: 1.82 us -> none  [on_device(): grad_down[None, :, padded - width:]]
    pallas_call x1 -> x0, other arithmetic: 1.22 us -> none  [on_device(): pl.pallas_call(functools.partial(kernel, experts), out_shape=(jax.ShapeDt...]
where the time goes in v2:
time: 100 us; the launch traced here: 99.9 us
  Pallas kernels  98.6 us (99%)
  between operations  1.29 us (1%)
    pallas_call x1, Pallas kernels, on_device(): pl.pallas_call(functools.partial(kernel, experts), out_shape=(vmem((width...  96.4 us
    pallas_call x1, Pallas kernels, on_device(): pl.pallas_call(store_kernel, out_shape=(jax.ShapeDtypeStruct((width, rows...  2.26 us

profile of v2, /device:TPU:1, one launch (start us, length us, event | category | flops | bytes accessed | tf_op | source)
XLA Modules:
  0.0 99.9 jit_solution(14558152801124765408)
XLA Ops:
  1.3 96.4 %shard_map.102 = (bf16[448,512]{1,0:T(8,128)(2,1)S(1)}, f32[1,512]{1,0:T(1,128)S(1)}, bf16[448,2048]{1,0:T(8,128)(2,1)S(1)}, bf16[448,1024]{1,0:T(8,128)(2,1)S(1)}) custom-call(s32[1]{0:T(128)S(6)} %copy.11.live_ref, bf16[448,512]{1,0:T(8,128)(2,1)} %bitcast.15, bf16[448,512]{1,0:T(8,128)(2,1)} %bitcast.16, f32[1,512]{1,0:T(1,128)} %bitcast.17, ...), custom_call_target="tpu_custom_call" | custom-call | tf_op jit(solution)/shard_map/pallas_call | solution.py:512
  97.7 2.3 %shard_map.103 = (bf16[448,512]{1,0:T(8,128)(2,1)}, bf16[512]{0:T(512)(128)(2,1)}, bf16[448,2048]{1,0:T(8,128)(2,1)}, bf16[448,1024]{1,0:T(8,128)(2,1)}) custom-call(bf16[448,512]{1,0:T(8,128)(2,1)S(1)} %get-tuple-element.12.rows_vm, f32[1,512]{1,0:T(1,128)S(1)} %get-tuple-element.13.prob_vm, bf16[448,2048]{1,0:T(8,128)(2,1)S(1)} %get-tuple-element.14.pair_vm, ...), custom_call_target="tpu_custom_call" | custom-call | tf_op jit(solution)/shard_map/pallas_call | solution.py:543

commit v3 on v2

--- a/solution.py
+++ b/solution.py
@@ -11,7 +11,8 @@
 BF16 = jnp.bfloat16
 MESH = pl.DeviceIdType.MESH
 BALANCE = 1.0
-PARTS = (2, 2, 1, 1)
+PARTS = (1, 2, 2, 1)
+COLUMN_FIRST = ()
 LANES = 128
 
 
@@ -110,10 +111,11 @@
 
     z = lax.rem(w, 8)
     xh = lax.div(w, 8)
-    wides = []
+    wides, even, odd = [], [], []
     for dx, dz in [(0, 4), (1, 4), (0, 3), (0, 5), (1, 3), (1, 5), (0, 2), (0, 6), (1, 2), (1, 6),
                    (0, 1), (0, 7), (1, 1), (1, 7), (1, 0)]:
         wides.append(lax.rem(xh + dx, 2) * 8 + lax.rem(z + dz, 8))
+        (even, odd)[dz % 2].append(wides[-1])
 
     barrier = pltpu.get_barrier_semaphore()
 
@@ -332,50 +334,92 @@
         piece = joined[c].at[core, at]
         to_y(k, piece, piece, send.at[c], recv.at[c])
 
+    cut_at = -(-joined[0].shape[3] // (2 * LANES)) * LANES
+
+    def piece_to_x(c, at):
+        piece = joined[c].at[core, at]
+        remote(piece, piece, gx_s.at[c], gx_r.at[c], w, other_x).start()
+
+    def half_to_y(c, k, at, first, size):
+        piece = joined[c].at[core, at, :, pl.ds(first, size)]
+        to_y(k, piece, piece, gf_s.at[c], gf_r.at[c])
+
     def forward(c):
+        if c in COLUMN_FIRST:
+            return
         await_bytes(joined[c].at[0, 0], gx_r.at[c])
         for k in (1, 3):
             piece_to_y(c, k, 2 * y + 1 - xl, gz_s, gz_r)
 
     def pass_near(c):
         await_bytes(joined[c].at[0, pl.ds(0, 2)], gy_r.at[c])
-        piece_to_y(c, 1, 2 * ys[3] + xl, gf_s, gf_r)
+        if c in COLUMN_FIRST:
+            half_to_y(c, 1, 2 * ys[3] + xl, 0, cut_at)
+            half_to_y(c, 3, 2 * ys[1] + xl, cut_at, joined[0].shape[3] - cut_at)
+            for k in (1, 3):
+                piece_to_x(c, 2 * ys[k] + xl)
+        else:
+            piece_to_y(c, 1, 2 * ys[3] + xl, gf_s, gf_r)
 
     def pass_far(c):
+        if c in COLUMN_FIRST:
+            await_bytes(joined[c].at[0, 0], gf_r.at[c])
+            piece_to_x(c, 2 * ys[2] + xl)
+            for k in range(4):
+                share(c, 2 * ys[k] + xl, 1)
+            return
         await_bytes(joined[c].at[0, pl.ds(0, 2)], gz_r.at[c])
         piece_to_y(c, 3, 2 * ys[1] + 1 - xl, gf_s, gf_r)
         for k in (0, 1, 3):
-            share(c, k)
-
-    def share(c, k):
-        pieces = joined[c].at[core, pl.ds(2 * ys[k], 2)]
+            share(c, 2 * ys[k], 2)
+
+    def share(c, at, count):
+        pieces = joined[c].at[core, pl.ds(at, count)]
         remote(pieces, pieces, gc_s.at[c], gc_r.at[c], w, other_core).start()
 
     def share_last(c):
+        if c in COLUMN_FIRST:
+            await_bytes(joined[c].at[0, pl.ds(0, 4)], gx_r.at[c])
+            for k in range(4):
+                share(c, 2 * ys[k] + 1 - xl, 1)
+            return
         await_bytes(joined[c].at[0, pl.ds(0, 2)], gf_r.at[c])
-        share(c, 2)
+        share(c, 2 * ys[2], 2)
 
     def give_back(c):
         slots = sizes[c]
         half_rows = both * slots
         await_bytes(joined[c].at[0], gc_r.at[c])
         cut = padded - LANES
-        for part in (0, 1):
-            pairs = joined[c][part, :, :, pl.ds(hidden, 2 * hidden)].reshape(half_rows, 2 * hidden)
-            inner = joined[c][part, :, :, pl.ds(3 * hidden, LANES)].reshape(half_rows, LANES)
-            value = product(pairs, w_pair[...], 1, 1)
-            ret_out[c][part, :, :, pl.ds(0, cut)] = (
-                value[:, :cut].astype(BF16).reshape(both, slots, cut)
+
+        def half(part, count):
+            at = pl.ds(part, count)
+            pairs = joined[c][at, :, :, pl.ds(hidden, 2 * hidden)]
+            inner = joined[c][at, :, :, pl.ds(3 * hidden, LANES)]
+            value = product(pairs.reshape(count * half_rows, 2 * hidden), w_pair[...], 1, 1)
+            ret_out[c][at, :, :, pl.ds(0, cut)] = (
+                value[:, :cut].astype(BF16).reshape(count, both, slots, cut)
             )
-            ret_out[c][part, :, :, pl.ds(cut, LANES)] = (
-                value[:, cut:].astype(BF16) + inner
-            ).reshape(both, slots, LANES)
-        ret_in[c][w] = ret_out[c][lax.rem(w, 2), lax.div(w, 2)]
-        for to in wides:
+            ret_out[c][at, :, :, pl.ds(cut, LANES)] = (
+                value[:, cut:].astype(BF16) + inner.reshape(count * half_rows, LANES)
+            ).reshape(count, both, slots, LANES)
+
+        def send(to):
             remote(
                 ret_out[c].at[lax.rem(to, 2), lax.div(to, 2)], ret_in[c].at[w],
                 ret_s.at[c], ret_r.at[c], to, g,
             ).start()
+
+        if half_rows < LANES:
+            half(0, 2)
+            for to in wides:
+                send(to)
+        else:
+            for number, group in enumerate((even, odd)):
+                half(lax.rem(z + number, 2), 1)
+                for to in group:
+                    send(to)
+        ret_in[c][w] = ret_out[c][lax.rem(w, 2), lax.div(w, 2)]
 
     def weigh():
         step = 256
@@ -411,11 +455,11 @@
 
     order = (
         (contract, 0), (reduce_y, 0), (relay_y, 0), (reduce_x, 0), (contract, 1), (reduce_y, 1),
-        (activate, 0), (relay_y, 1), (contract, 2), (reduce_y, 2), (forward, 0), (pass_near, 0),
-        (contract, 3), (reduce_y, 3), (reduce_x, 1), (relay_y, 2), (pass_far, 0), (activate, 1),
-        (relay_y, 3), (share_last, 0), (forward, 1), (reduce_x, 2), (give_back, 0), (activate, 2),
-        (pass_near, 1), (pass_far, 1), (reduce_x, 3), (activate, 3), (forward, 2),
-        (share_last, 1), (forward, 3), (give_back, 1), (pass_near, 2), (pass_near, 3),
+        (activate, 0), (relay_y, 1), (forward, 0), (pass_near, 0), (contract, 2), (reduce_y, 2),
+        (reduce_x, 1), (pass_far, 0), (contract, 3), (reduce_y, 3), (relay_y, 2), (activate, 1),
+        (relay_y, 3), (share_last, 0), (forward, 1), (reduce_x, 2), (give_back, 0),
+        (pass_near, 1), (reduce_x, 3), (activate, 2), (pass_far, 1), (activate, 3), (forward, 2),
+        (share_last, 1), (give_back, 1), (forward, 3), (pass_near, 2), (pass_near, 3),
         (pass_far, 2), (pass_far, 3), (share_last, 2), (share_last, 3), (give_back, 2),
         (give_back, 3),
     )
@@ -446,9 +490,14 @@
         await_bytes(far_out[c], far_s.at[c])
         await_bytes(y_out[c], y_s.at[c])
         await_bytes(x_out[c], x_s.at[c])
-        await_bytes(joined[c].at[0, 0], gx_s.at[c])
-        for sem in (gy_s, gz_s, gf_s):
-            await_bytes(joined[c].at[0, pl.ds(0, 2)], sem.at[c])
+        await_bytes(joined[c].at[0, pl.ds(0, 2)], gy_s.at[c])
+        if c in COLUMN_FIRST:
+            await_bytes(joined[c].at[0, pl.ds(0, 4)], gx_s.at[c])
+            await_bytes(joined[c].at[0, 0], gf_s.at[c])
+        else:
+            await_bytes(joined[c].at[0, 0], gx_s.at[c])
+            await_bytes(joined[c].at[0, pl.ds(0, 2)], gz_s.at[c])
+            await_bytes(joined[c].at[0, pl.ds(0, 2)], gf_s.at[c])
         await_bytes(joined[c].at[0], gc_s.at[c])
         await_bytes(outgoing[c].at[pl.ds(0, len(wides)), :, pl.ds(0, padded)], ret_s.at[c])
 

time: 100 us -> 97.7 us (0.977)
  Pallas kernels: 98.6 us -> 96.3 us
    pallas_call x1, Pallas kernels: 96.4 us -> 94 us  [on_device(): pl.pallas_call(functools.partial(kernel, experts), out_shape=(vmem((width...]
where the time goes in v3:
time: 97.7 us; the launch traced here: 97.6 us
  Pallas kernels  96.3 us (99%)
  between operations  1.29 us (1%)
    pallas_call x1, Pallas kernels, on_device(): pl.pallas_call(functools.partial(kernel, experts), out_shape=(vmem((width...  94 us
    pallas_call x1, Pallas kernels, on_device(): pl.pallas_call(store_kernel, out_shape=(jax.ShapeDtypeStruct((width, rows...  2.26 us

profile of v3, /device:TPU:1, one launch (start us, length us, event | category | flops | bytes accessed | tf_op | source)
XLA Modules:
  0.0 97.6 jit_solution(2028133273127728109)
XLA Ops:
  1.3 94.0 %shard_map.102 = (bf16[448,512]{1,0:T(8,128)(2,1)S(1)}, f32[1,512]{1,0:T(1,128)S(1)}, bf16[448,2048]{1,0:T(8,128)(2,1)S(1)}, bf16[448,1024]{1,0:T(8,128)(2,1)S(1)}) custom-call(s32[1]{0:T(128)S(6)} %copy.11.live_ref, bf16[448,512]{1,0:T(8,128)(2,1)} %bitcast.15, bf16[448,512]{1,0:T(8,128)(2,1)} %bitcast.16, f32[1,512]{1,0:T(1,128)} %bitcast.17, ...), custom_call_target="tpu_custom_call" | custom-call | tf_op jit(solution)/shard_map/pallas_call | solution.py:561
  95.3 2.3 %shard_map.103 = (bf16[448,512]{1,0:T(8,128)(2,1)}, bf16[512]{0:T(512)(128)(2,1)}, bf16[448,2048]{1,0:T(8,128)(2,1)}, bf16[448,1024]{1,0:T(8,128)(2,1)}) custom-call(bf16[448,512]{1,0:T(8,128)(2,1)S(1)} %get-tuple-element.12.rows_vm, f32[1,512]{1,0:T(1,128)S(1)} %get-tuple-element.13.prob_vm, bf16[448,2048]{1,0:T(8,128)(2,1)S(1)} %get-tuple-element.14.pair_vm, ...), custom_call_target="tpu_custom_call" | custom-call | tf_op jit(solution)/shard_map/pallas_call | solution.py:592
